TPU v7x, 256 devices: a whole 4x4x8 slice. The times are simulated.
256 devices in a mesh: frames: 16 (over x, y), pix: 16 (over z, core).
Axes of the slice: x: 4, y: 4, z: 8, core: 2. Of those that a mesh axis runs over, the one named last changes fastest.
Arguments:
- intensity: bfloat16 [512, 1048576], P('frames', 'pix'), may hold values from -6 to 6
- chi_bin: int32 [1048576], P('pix'), may hold values from 0 to 255
- split: float32 [1048576], P('pix'), may hold values from 0 to 1
- mask: int32 [1048576], P('pix'), may hold values 0 or 1
- tile_row: int32 [8192], P('pix'), may hold values from 0 to 255
Outputs:
- correlation: float32 [256, 2, 128, 256], P('frames', None, 'pix')
All inputs are finite; a program needn't handle non-finite values. No bound on the sum of `mask` on one device may be relied on, other than what follows from the above.
Results may differ from a plain program's by a relative error of at most 0.0027.
Values sent between devices are 32-bit elements; how exact they have to be, the bound alone decides.
A program may use at most 128 MiB of HBM per device.

v0:
```python
import math

import jax
import jax.numpy as jnp
from jax import lax
from jax.sharding import PartitionSpec as P

NQ = 256
NCHI = 256
NH = 128


def in_one_piece(arrays, axis, dim, along):
    ends, at = ([], 0)
    for a in arrays[:-1]:
        at += a.shape[along]
        ends.append(at)
    both = jnp.concatenate(arrays, axis=along)
    return tuple(
        jnp.split(lax.psum_scatter(both, axis, scatter_dimension=dim, tiled=True), ends, axis=along)
    )


def fourier_table():
    harmonic = lax.iota(jnp.int32, NH)[:, None]
    column = lax.iota(jnp.int32, NCHI)[None, :]
    phases = (harmonic * column % NCHI).astype(jnp.float32) * (2.0 * math.pi / NCHI)
    factor = 1.0 / math.sqrt(NCHI)
    return jnp.stack([jnp.cos(phases) * factor, -jnp.sin(phases) * factor], 0)


def body(intensity, chi_bin, split, mask, tile_row):
    frames_dev = intensity.shape[0]
    tiles = tile_row.shape[0]
    tile_block = math.gcd(tiles, 128)
    block_count = tiles // tile_block
    high = lax.Precision.HIGHEST
    usable = mask.astype(jnp.float32)
    near_weight = (usable * split).astype(jnp.bfloat16)
    far_weight = (usable * (1.0 - split)).astype(jnp.bfloat16)
    next_chi = (chi_bin + 1) % NCHI
    columns = lax.iota(jnp.int32, NCHI)
    cycles = lax.iota(jnp.int32, NQ)
    nothing = jnp.zeros((), jnp.bfloat16)
    width = tile_block * 128

    def accumulate(block_index, state_pair):
        partial_cake, counts = state_pair
        first_pixel = block_index * width
        chi_rows = lax.dynamic_slice_in_dim(chi_bin, first_pixel, width).reshape(tile_block, 128, 1)
        next_rows = lax.dynamic_slice_in_dim(next_chi, first_pixel, width).reshape(
            tile_block, 128, 1
        )
        near_rows = lax.dynamic_slice_in_dim(near_weight, first_pixel, width).reshape(
            tile_block, 128, 1
        )
        far_rows = lax.dynamic_slice_in_dim(far_weight, first_pixel, width).reshape(
            tile_block, 128, 1
        )
        tile_rows = lax.dynamic_slice_in_dim(tile_row, block_index * tile_block, tile_block)
        weights = jnp.where(chi_rows == columns, near_rows, nothing) + jnp.where(
            next_rows == columns, far_rows, nothing
        )
        pixels = lax.dynamic_slice_in_dim(intensity, first_pixel, width, 1).reshape(
            frames_dev, tile_block, 128
        )
        partial_value = jnp.einsum(
            "ftp,tpc->ftc", pixels, weights, preferred_element_type=jnp.float32
        )
        rows_hot = (tile_rows[:, None] == cycles[None, :]).astype(jnp.float32)
        partial_cake = partial_cake + jnp.einsum(
            "ftc,tq->fqc", partial_value, rows_hot, precision=high
        )
        totals = jnp.sum(weights.astype(jnp.float32), axis=1)
        counts = counts + jnp.einsum("tc,tq->qc", totals, rows_hot, precision=high)
        return (partial_cake, counts)

    start_pair = (
        jnp.zeros((frames_dev, NQ, NCHI), jnp.float32),
        jnp.zeros((NQ, NCHI), jnp.float32),
    )
    partial_cake, counts = lax.fori_loop(0, block_count, accumulate, start_pair)
    table = fourier_table()
    cake_block, count_block = in_one_piece((partial_cake, counts[None]), "pix", 1, 0)
    normed = cake_block / jnp.maximum(count_block, 1.0)
    local_spectra = jnp.einsum("fqc,rnc->frnq", normed, table, precision=high)
    spectra = lax.all_to_all(local_spectra, "pix", split_axis=2, concat_axis=3, tiled=True)
    frame_scale = 1.0 / math.sqrt(frames_dev * lax.axis_size("frames"))
    real_part = spectra[:, 0]
    imag_part = spectra[:, 1]
    real_corr = jnp.einsum("fnq,fnp->qnp", real_part, real_part, precision=high) + jnp.einsum(
        "fnq,fnp->qnp", imag_part, imag_part, precision=high
    )
    imag_corr = jnp.einsum("fnq,fnp->qnp", imag_part, real_part, precision=high) - jnp.einsum(
        "fnq,fnp->qnp", real_part, imag_part, precision=high
    )
    return lax.psum_scatter(
        jnp.stack([real_corr, imag_corr], 1) * frame_scale,
        "frames",
        scatter_dimension=0,
        tiled=True,
    )


def solution(mesh):
    in_specs = (P("frames", "pix"), P("pix"), P("pix"), P("pix"), P("pix"))
    out_specs = P("frames", None, "pix", None)
    return jax.shard_map(body, mesh=mesh, in_specs=in_specs, out_specs=out_specs, check_vma=False)
```

profile of v0, /device:TPU:1, one launch (start us, length us, event | category | flops | bytes accessed | tf_op | source)
XLA Modules:
  0.0 389.9 jit_solution(7500786866274454249)
XLA Ops:
  6.5 0.0 reduce-scatter.3.cloned.1.call-start
  6.5 1.1 add_select_fusion
  7.6 1.1 multiply_convert_fusion
  8.7 166.3 %while.18 = (s32[]{:T(128)}, f32[32,256,256]{2,1,0:T(8,128)}, f32[256,256]{1,0:T(8,128)S(1)}, s32[512]{0:T(512)}, s32[65536]{0:T(1024)}, /*index=5*/bf16[65536]{...) while((s32[]{:T(128)}, f32[32,256,256]{2,1,0:T(8,128)}, ...), condition=%wide.region_2.3_spmd.clone.clone, body=%wide.region_0.2_spmd.clone.clone.sunk | while | flops 3665985536 | bytes 27789568 | solution.py:82
  8.7 0.9 dynamic-slice_bitcast_fusion.14
  9.6 13.3 %fusion.57 = f32[32,128,256]{2,0,1:T(8,128)} fusion(s32[128,128]{1,0:T(8,128)S(1)} %get-tuple-element.353, s32[128,128]{1,0:T(8,128)S(1)} %get-tuple-element.354, bf16[128,128]{1,0:T(8,128)(2,1)S(1)} %get-tuple-element.355, bf16[128,128]{1,0:T(8,128)(2,1)S(1)} %get-tuple-element.356, bf16[32,65536]{1,0:T(8,128)(2,1)} %get-tuple-element.395, ...), kind=kOutput, calls=%fused_computation.14.clone.3 | convolution fusion | flops 301989888 | bytes 5439492 | tf_op jit(solution)/shard_map/while/body/eval_jaxpr/ftp,tpc->ftc/dot_general | solution.py:67
  22.9 0.8 dynamic_slice.77
  23.7 13.7 %bitcast_add_fusion.2 = f32[32,256,256]{2,1,0:T(8,128)} fusion(f32[32,256,256]{2,1,0:T(8,128)} %get-tuple-element.373, pred[]{:T(512)S(6)} %compare.14, f32[32,128,256]{2,0,1:T(8,128)} %fusion.57, s32[128]{0:T(128)S(1)} %dynamic_slice.77), kind=kOutput, calls=%fused_computation.7.clone.1 | convolution fusion | flops 3225452544 | bytes 20972032 | tf_op jit(solution)/shard_map/while/body/eval_jaxpr/ftc,tq->fqc/dot_general | solution.py:71
  37.4 11.5 %convert_reduce_fusion.2 = f32[128,256]{1,0:T(8,128)S(1)} fusion(s32[128,128]{1,0:T(8,128)S(1)} %get-tuple-element.353, s32[128,128]{1,0:T(8,128)S(1)} %get-tuple-element.354, bf16[128,128]{1,0:T(8,128)(2,1)S(1)} %get-tuple-element.355, bf16[128,128]{1,0:T(8,128)(2,1)S(1)} %get-tuple-element.356), kind=kLoop, calls=%fused_computation.3.clone.1 | loop fusion | flops 37715968 | bytes 327680 | tf_op jit(solution)/shard_map/while/body/eval_jaxpr/reduce_sum | solution.py:74
  48.9 0.3 convolution_add_fusion.2
  49.3 0.9 dynamic-slice_bitcast_fusion.14
  50.2 13.3 %fusion.57 = f32[32,128,256]{2,0,1:T(8,128)} fusion(s32[128,128]{1,0:T(8,128)S(1)} %get-tuple-element.353, s32[128,128]{1,0:T(8,128)S(1)} %get-tuple-element.354, bf16[128,128]{1,0:T(8,128)(2,1)S(1)} %get-tuple-element.355, bf16[128,128]{1,0:T(8,128)(2,1)S(1)} %get-tuple-element.356, bf16[32,65536]{1,0:T(8,128)(2,1)} %get-tuple-element.395, ...), kind=kOutput, calls=%fused_computation.14.clone.3 | convolution fusion | flops 301989888 | bytes 5439492 | tf_op jit(solution)/shard_map/while/body/eval_jaxpr/ftp,tpc->ftc/dot_general | solution.py:67
  63.5 0.8 dynamic_slice.77
  64.3 15.0 %bitcast_add_fusion.2 = f32[32,256,256]{2,1,0:T(8,128)} fusion(f32[32,256,256]{2,1,0:T(8,128)} %get-tuple-element.373, pred[]{:T(512)S(6)} %compare.14, f32[32,128,256]{2,0,1:T(8,128)} %fusion.57, s32[128]{0:T(128)S(1)} %dynamic_slice.77), kind=kOutput, calls=%fused_computation.7.clone.1 | convolution fusion | flops 3225452544 | bytes 20972032 | tf_op jit(solution)/shard_map/while/body/eval_jaxpr/ftc,tq->fqc/dot_general | solution.py:71
  79.3 11.5 %convert_reduce_fusion.2 = f32[128,256]{1,0:T(8,128)S(1)} fusion(s32[128,128]{1,0:T(8,128)S(1)} %get-tuple-element.353, s32[128,128]{1,0:T(8,128)S(1)} %get-tuple-element.354, bf16[128,128]{1,0:T(8,128)(2,1)S(1)} %get-tuple-element.355, bf16[128,128]{1,0:T(8,128)(2,1)S(1)} %get-tuple-element.356), kind=kLoop, calls=%fused_computation.3.clone.1 | loop fusion | flops 37715968 | bytes 327680 | tf_op jit(solution)/shard_map/while/body/eval_jaxpr/reduce_sum | solution.py:74
  90.8 0.3 convolution_add_fusion.2
  91.2 0.9 dynamic-slice_bitcast_fusion.14
  92.1 13.3 %fusion.57 = f32[32,128,256]{2,0,1:T(8,128)} fusion(s32[128,128]{1,0:T(8,128)S(1)} %get-tuple-element.353, s32[128,128]{1,0:T(8,128)S(1)} %get-tuple-element.354, bf16[128,128]{1,0:T(8,128)(2,1)S(1)} %get-tuple-element.355, bf16[128,128]{1,0:T(8,128)(2,1)S(1)} %get-tuple-element.356, bf16[32,65536]{1,0:T(8,128)(2,1)} %get-tuple-element.395, ...), kind=kOutput, calls=%fused_computation.14.clone.3 | convolution fusion | flops 301989888 | bytes 5439492 | tf_op jit(solution)/shard_map/while/body/eval_jaxpr/ftp,tpc->ftc/dot_general | solution.py:67
  105.4 0.8 dynamic_slice.77
  106.2 15.0 %bitcast_add_fusion.2 = f32[32,256,256]{2,1,0:T(8,128)} fusion(f32[32,256,256]{2,1,0:T(8,128)} %get-tuple-element.373, pred[]{:T(512)S(6)} %compare.14, f32[32,128,256]{2,0,1:T(8,128)} %fusion.57, s32[128]{0:T(128)S(1)} %dynamic_slice.77), kind=kOutput, calls=%fused_computation.7.clone.1 | convolution fusion | flops 3225452544 | bytes 20972032 | tf_op jit(solution)/shard_map/while/body/eval_jaxpr/ftc,tq->fqc/dot_general | solution.py:71
  121.2 11.5 %convert_reduce_fusion.2 = f32[128,256]{1,0:T(8,128)S(1)} fusion(s32[128,128]{1,0:T(8,128)S(1)} %get-tuple-element.353, s32[128,128]{1,0:T(8,128)S(1)} %get-tuple-element.354, bf16[128,128]{1,0:T(8,128)(2,1)S(1)} %get-tuple-element.355, bf16[128,128]{1,0:T(8,128)(2,1)S(1)} %get-tuple-element.356), kind=kLoop, calls=%fused_computation.3.clone.1 | loop fusion | flops 37715968 | bytes 327680 | tf_op jit(solution)/shard_map/while/body/eval_jaxpr/reduce_sum | solution.py:74
  132.7 0.3 convolution_add_fusion.2
  133.1 0.9 dynamic-slice_bitcast_fusion.14
  134.0 13.3 %fusion.57 = f32[32,128,256]{2,0,1:T(8,128)} fusion(s32[128,128]{1,0:T(8,128)S(1)} %get-tuple-element.353, s32[128,128]{1,0:T(8,128)S(1)} %get-tuple-element.354, bf16[128,128]{1,0:T(8,128)(2,1)S(1)} %get-tuple-element.355, bf16[128,128]{1,0:T(8,128)(2,1)S(1)} %get-tuple-element.356, bf16[32,65536]{1,0:T(8,128)(2,1)} %get-tuple-element.395, ...), kind=kOutput, calls=%fused_computation.14.clone.3 | convolution fusion | flops 301989888 | bytes 5439492 | tf_op jit(solution)/shard_map/while/body/eval_jaxpr/ftp,tpc->ftc/dot_general | solution.py:67
  147.3 0.8 dynamic_slice.77
  148.1 15.0 %bitcast_add_fusion.2 = f32[32,256,256]{2,1,0:T(8,128)} fusion(f32[32,256,256]{2,1,0:T(8,128)} %get-tuple-element.373, pred[]{:T(512)S(6)} %compare.14, f32[32,128,256]{2,0,1:T(8,128)} %fusion.57, s32[128]{0:T(128)S(1)} %dynamic_slice.77), kind=kOutput, calls=%fused_computation.7.clone.1 | convolution fusion | flops 3225452544 | bytes 20972032 | tf_op jit(solution)/shard_map/while/body/eval_jaxpr/ftc,tq->fqc/dot_general | solution.py:71
  163.0 11.5 %convert_reduce_fusion.2 = f32[128,256]{1,0:T(8,128)S(1)} fusion(s32[128,128]{1,0:T(8,128)S(1)} %get-tuple-element.353, s32[128,128]{1,0:T(8,128)S(1)} %get-tuple-element.354, bf16[128,128]{1,0:T(8,128)(2,1)S(1)} %get-tuple-element.355, bf16[128,128]{1,0:T(8,128)(2,1)S(1)} %get-tuple-element.356), kind=kLoop, calls=%fused_computation.3.clone.1 | loop fusion | flops 37715968 | bytes 327680 | tf_op jit(solution)/shard_map/while/body/eval_jaxpr/reduce_sum | solution.py:74
  174.6 0.3 convolution_add_fusion.2
  174.9 7.6 %pad_maximum_fusion = f32[33,256,256]{2,1,0:T(8,128)} fusion(f32[1,256,256]{2,1,0:T(8,128)S(1)} %bitcast.96, f32[32,256,256]{2,1,0:T(8,128)} %get-tuple-element.209), kind=kLoop, calls=%fused_computation.28 | loop fusion | flops 2162688 | bytes 17301504 | tf_op jit(solution)/shard_map/concatenate | solution.py:18
  182.6 0.0 reduce-scatter.3.cloned.1.call-update
  182.6 0.0 reduce-scatter.5.cloned.1.call-start
  182.7 0.5 negate_multiply_fusion
  183.2 71.9 %reduce-scatter.3.cloned.1.call-done = f32[33,16,256]{2,1,0:T(8,128)} async-done(((f32[33,256,256]{2,1,0:T(8,128)}), f32[33,16,256]{2,1,0:T(8,128)}) %reduce-scatter.3.cloned.1.call-update) | async-done | bytes 540688 | tf_op jit(solution)/shard_map/reduce_scatter | solution.py:20
  255.1 0.7 fusion.37
  255.8 1.1 slice_divide_fusion
  256.9 0.8 convolution_bitcast_fusion
  257.7 1.8 copy.26
  259.6 0.9 reshape.105
  260.5 25.2 %all_to_all.18 = f32[16,1,8192]{2,1,0:T(1,128)S(1)} all-to-all(f32[16,1,8192]{2,1,0:T(1,128)S(1)} %reshape.105), channel_id=1, replica_groups=mesh['frames'=16,'pix'=16] {'pix'}, dimensions={0} | all-to-all | bytes 1048576 | tf_op jit(solution)/shard_map/all_to_all | solution.py:87
  285.7 0.5 broadcast.129
  286.2 1.9 reduce
  288.1 0.7 reshape.106
  288.8 0.2 copy.28
  289.0 1.9 fusion.25
  290.8 1.9 fusion.24
  292.7 2.0 add_bitcast_fusion
  294.7 2.0 subtract_bitcast_fusion
  296.7 2.4 maximum_multiply_fusion
  299.1 5.5 %copy.31 = f32[256,2,8,256]{3,2,1,0:T(8,128)} copy(f32[256,2,8,256]{0,3,2,1:T(8,128)} %maximum_multiply_fusion) | data formatting | bytes 8388608 | tf_op jit(solution)/shard_map/mul | solution.py:98
  304.6 0.0 reduce-scatter.5.cloned.1.call-update
  304.6 78.5 %reduce-scatter.5.cloned.1.call-done = f32[16,2,8,256]{3,2,1,0:T(8,128)} async-done(((f32[256,2,8,256]{3,2,1,0:T(8,128)}), f32[16,2,8,256]{3,2,1,0:T(8,128)}) %reduce-scatter.5.cloned.1.call-update) | async-done | bytes 262160 | tf_op jit(solution)/shard_map/reduce_scatter | solution.py:97
  (6 shorter events, 0.1 us)
Async XLA Ops:
  6.5 248.5 %reduce-scatter.3.cloned.1.call-start = ((), (), s32[]{:S(2)}) async-start(), calls=%async_computation.3 | async-start | bytes 9191424 | tf_op jit(solution)/shard_map/reduce_scatter | solution.py:20
  182.6 200.5 %reduce-scatter.5.cloned.1.call-start = ((), (), s32[]{:S(2)}) async-start(), calls=%async_computation.4 | async-start | bytes 4456448 | tf_op jit(solution)/shard_map/reduce_scatter | solution.py:97
Sparse Core Ops, SparseCore 0:
  182.7 72.2 reduce-scatter.2
  304.7 78.3 reduce-scatter.4
where the time goes:
time: 391 us; the launch traced here: 390 us
  waiting for transfers between devices  150 us (38%)
  matrix products  122 us (31%)
  other arithmetic  62.5 us (16%)
  blocking collectives  25.2 us (6%)
  local copies, waits for them, and re-layouts  16.1 us (4%)
  between operations  13.5 us (3%)
    reduce_scatter x1, waiting for transfers between devices, body(): lax.psum_scatter(jnp.stack([real_corr, imag_corr], 1) * frame_scale, 'fra...  78.5 us
    reduce_scatter x1, waiting for transfers between devices, in_one_piece(): lax.psum_scatter(both, axis, scatter_dimension=dim, tiled=True)  71.9 us
    dot_general x4, matrix products, accumulate(): jnp.einsum('ftc,tq->fqc', partial_value, rows_hot, precision=high)  58.7 us
    dot_general x4, matrix products, accumulate(): jnp.einsum('ftp,tpc->ftc', pixels, weights, preferred_element_type=jnp.fl...  53.4 us
    reduce_sum x4, other arithmetic, accumulate(): totals = jnp.sum(weights.astype(jnp.float32), axis=1)  46.1 us
    all_to_all x1, blocking collectives, body(): lax.all_to_all(local_spectra, 'pix', split_axis=2, concat_axis=3, tiled=T...  25.2 us
  transfers between devices with their start and end apart: 2, of which 2 were waited for; matrix products, arithmetic and copies ran while one was open for 0% of the time, Pallas kernels for 0%

commit v1 on v0

v1 whole, which is shorter than its diff:
```python
import math

import jax
import jax.numpy as jnp
from jax import lax
from jax.experimental import pallas as pl
from jax.experimental.pallas import tpu as pltpu
from jax.sharding import PartitionSpec as P

NQ = 256
NCHI = 256
NH = 128
ROWS = 40
TILE_BLOCK = 128
GROUP = 16


def bin_kernel(tiles_block, rows_ref, x_ref, chi_ref, split_ref, mask_ref, cake_ref, acc, vals, sem):
    step = pl.program_id(0)
    frames = x_ref.shape[0]
    bf = jnp.bfloat16

    @pl.when(step == 0)
    def _():
        acc[...] = jnp.zeros_like(acc)
        vals[...] = jnp.zeros_like(vals)

    zero = jnp.zeros((), bf)
    columns = lax.broadcasted_iota(jnp.int32, (NCHI, 128), 0).astype(jnp.float32).astype(bf)
    row = lax.broadcasted_iota(jnp.int32, (16, 256), 0)
    lane = lax.broadcasted_iota(jnp.int32, (16, 256), 1)
    ones = jnp.where(((row == 0) & (lane < 128)) | ((row == 8) & (lane >= 128)), 1.0, 0.0).astype(bf)
    blank = jnp.zeros((frames, 128), bf)

    def weights_of(t):
        chi = chi_ref[pl.ds(t, 1), :]
        usable = mask_ref[pl.ds(t, 1), :].astype(jnp.float32)
        split = split_ref[pl.ds(t, 1), :]
        near = (usable * split).astype(bf)
        far = (usable * (1.0 - split)).astype(bf)
        here = chi.astype(jnp.float32).astype(bf)
        after = ((chi + 1) & (NCHI - 1)).astype(jnp.float32).astype(bf)
        return jnp.where(columns == here, near, jnp.where(columns == after, far, zero))

    def group(g, carry):
        slot = lax.rem(g, 2)
        for u in range(0, GROUP, 2):
            t = g * GROUP + u
            weights = jnp.concatenate([weights_of(t), weights_of(t + 1)], axis=1)
            a = x_ref[:, pl.ds(pl.multiple_of(t * 128, 128), 128)]
            b = x_ref[:, pl.ds(pl.multiple_of(t * 128 + 128, 128), 128)]
            left = jnp.concatenate(
                [jnp.concatenate([a, blank], 1), jnp.concatenate([blank, b], 1), ones], axis=0
            )
            value = lax.dot_general(
                left, weights, (((1,), (1,)), ((), ())), preferred_element_type=jnp.float32
            )
            vals[slot, u, :frames] = value[:frames]
            vals[slot, u, frames:] = value[2 * frames:2 * frames + 8]
            vals[slot, u + 1, :frames] = value[frames:2 * frames]
            vals[slot, u + 1, frames:] = value[2 * frames + 8:]
        before = jnp.maximum(step * tiles_block + (g - 1) * GROUP, 0)
        for u in range(GROUP):
            q = rows_ref[before + u]
            acc[q] = acc[q] + vals[1 - slot, u]
        return carry

    groups = tiles_block // GROUP
    lax.fori_loop(0, groups, group, 0)

    @pl.when(step == pl.num_programs(0) - 1)
    def _():
        for u in range(GROUP):
            q = rows_ref[(step + 1) * tiles_block - GROUP + u]
            acc[q] = acc[q] + vals[(groups - 1) % 2, u]
        copy = pltpu.make_async_copy(acc, cake_ref, sem)
        copy.start()
        copy.wait()


def binned(intensity, chi_bin, split, mask, tile_row):
    frames = intensity.shape[0]
    tiles = tile_row.shape[0]
    block = TILE_BLOCK
    flat = pl.BlockSpec((block, 128), lambda i, rows: (i, 0))
    return pl.pallas_call(
        lambda *refs: bin_kernel(block, *refs),
        out_shape=jax.ShapeDtypeStruct((NQ, ROWS, NCHI), jnp.float32),
        grid_spec=pltpu.PrefetchScalarGridSpec(
            num_scalar_prefetch=1,
            grid=(tiles // block,),
            in_specs=[pl.BlockSpec((frames, block * 128), lambda i, rows: (0, i)), flat, flat, flat],
            out_specs=pl.BlockSpec(memory_space=pl.ANY),
            scratch_shapes=[
                pltpu.VMEM((NQ, ROWS, NCHI), jnp.float32),
                pltpu.VMEM((2, GROUP, ROWS, NCHI), jnp.float32),
                pltpu.SemaphoreType.DMA,
            ],
        ),
        compiler_params=pltpu.CompilerParams(
            dimension_semantics=("arbitrary",), vmem_limit_bytes=40 << 20
        ),
        name="binning",
    )(tile_row, intensity, *(a.reshape(tiles, 128) for a in (chi_bin, split, mask)))


def fourier_table():
    harmonic = lax.iota(jnp.int32, NH)[:, None]
    column = lax.iota(jnp.int32, NCHI)[None, :]
    phases = (harmonic * column % NCHI).astype(jnp.float32) * (2.0 * math.pi / NCHI)
    factor = 1.0 / math.sqrt(NCHI)
    return jnp.stack([jnp.cos(phases) * factor, -jnp.sin(phases) * factor], 0)


def body(intensity, chi_bin, split, mask, tile_row):
    frames_dev = intensity.shape[0]
    high = lax.Precision.HIGHEST
    cake = binned(intensity, chi_bin, split, mask, tile_row)[:, :frames_dev + 1]
    block = lax.psum_scatter(cake, "pix", scatter_dimension=0, tiled=True)
    normed = block[:, :frames_dev] / jnp.maximum(block[:, frames_dev:], 1.0)
    local_spectra = jnp.einsum("qfc,rnc->frnq", normed, fourier_table(), precision=high)
    spectra = lax.all_to_all(local_spectra, "pix", split_axis=2, concat_axis=3, tiled=True)
    frame_scale = 1.0 / math.sqrt(frames_dev * lax.axis_size("frames"))
    real_part = spectra[:, 0]
    imag_part = spectra[:, 1]
    real_corr = jnp.einsum("fnq,fnp->qnp", real_part, real_part, precision=high) + jnp.einsum(
        "fnq,fnp->qnp", imag_part, imag_part, precision=high
    )
    imag_corr = jnp.einsum("fnq,fnp->qnp", imag_part, real_part, precision=high) - jnp.einsum(
        "fnq,fnp->qnp", real_part, imag_part, precision=high
    )
    return lax.psum_scatter(
        jnp.stack([real_corr, imag_corr], 1) * frame_scale,
        "frames",
        scatter_dimension=0,
        tiled=True,
    )


def solution(mesh):
    in_specs = (P("frames", "pix"), P("pix"), P("pix"), P("pix"), P("pix"))
    out_specs = P("frames", None, "pix", None)
    return jax.shard_map(body, mesh=mesh, in_specs=in_specs, out_specs=out_specs, check_vma=False)
```

time: 391 us -> 246 us (0.63)
  matrix products: 122 us -> 9.33 us
  other arithmetic: 62.5 us -> 5.76 us
  Pallas kernels: 0 us -> 21.8 us
  waiting for transfers between devices: 150 us -> 154 us
    dot_general x13 -> x1, matrix products: 114 us -> 1.66 us  [body(): jnp.einsum('qfc,rnc->frnq', normed, fourier_table(), precision=high)]
    reduce_sum x4 -> x0, other arithmetic: 46.1 us -> none  [accumulate(): totals = jnp.sum(weights.astype(jnp.float32), axis=1)]
    pallas_call x0 -> x1, Pallas kernels: none -> 21.8 us  [binned(): pl.pallas_call(lambda *refs: bin_kernel(block, *refs), out_shape=jax.Shap...]
    concatenate x1 -> x0, other arithmetic: 7.64 us -> none  [in_one_piece(): both = jnp.concatenate(arrays, axis=along)]
    unnamed x2 -> x13, local copies, waits for them, and re-layouts: 1.6 us -> 7.32 us
where the time goes in v1:
time: 246 us; the launch traced here: 245 us
  waiting for transfers between devices  154 us (63%)
  blocking collectives  25.2 us (10%)
  Pallas kernels  21.8 us (9%)
  local copies, waits for them, and re-layouts  15.3 us (6%)
  between operations  13.5 us (5%)
  matrix products  9.33 us (4%)
  other arithmetic  5.76 us (2%)
    reduce_scatter x1, waiting for transfers between devices, body(): lax.psum_scatter(jnp.stack([real_corr, imag_corr], 1) * frame_scale, 'fra...  78.4 us
    reduce_scatter x1, waiting for transfers between devices, body(): block = lax.psum_scatter(cake, 'pix', scatter_dimension=0, tiled=True)  75.5 us
    all_to_all x1, blocking collectives, body(): lax.all_to_all(local_spectra, 'pix', split_axis=2, concat_axis=3, tiled=T...  25.2 us
    pallas_call x1, Pallas kernels, binned(): pl.pallas_call(lambda *refs: bin_kernel(block, *refs), out_shape=jax.Shap...  21.8 us
    unnamed x13, local copies, waits for them, and re-layouts  7.32 us
    mul x1, local copies, waits for them, and re-layouts, body(): jnp.stack([real_corr, imag_corr], 1) * frame_scale  5.48 us
  transfers between devices with their start and end apart: 2, of which 2 were waited for; matrix products, arithmetic and copies ran while one was open for 0% of the time, Pallas kernels for 0%

profile of v1, /device:TPU:1, one launch (start us, length us, event | category | flops | bytes accessed | tf_op | source)
XLA Modules:
  0.0 245.0 jit_solution(1868832850732674402)
XLA Ops:
  6.5 0.0 reduce-scatter.3.cloned.1.call-start
  6.5 0.0 copy-start
  6.5 2.2 copy-done
  8.7 0.0 copy-start.1
  8.7 0.9 copy-done.1
  9.7 0.0 copy-start.2
  9.7 0.9 copy-done.2
  10.6 0.0 copy-start.3
  10.6 0.9 copy-done.3
  11.6 0.0 copy-start.4
  11.6 0.7 copy-done.4
  12.3 21.8 %binning.1 = f32[256,40,256]{2,1,0:T(8,128)} custom-call(s32[512]{0:T(512)S(1)} %copy-done.4, bf16[32,65536]{1,0:T(8,128)(2,1)S(1)} %copy-done, s32[512,128]{1,0:T(8,128)S(1)} %bitcast.49, f32[512,128]{1,0:T(8,128)S(1)} %bitcast.50, s32[512,128]{1,0:T(8,128)S(1)} %bitcast.51), custom_call_target="tpu_custom_call" | custom-call | tf_op jit(solution)/shard_map/binning/pallas_call | solution.py:86
  34.1 0.0 reduce-scatter.3.cloned.1.call-update
  34.1 0.0 reduce-scatter.5.cloned.1.call-start
  34.1 0.5 negate_multiply_fusion
  34.7 75.5 %reduce-scatter.3.cloned.1.call-done = f32[16,33,256]{2,1,0:T(8,128)} async-done(((f32[256,33,256]{2,1,0:T(8,128)}), f32[16,33,256]{2,1,0:T(8,128)}) %reduce-scatter.3.cloned.1.call-update) | async-done | bytes 540688 | tf_op jit(solution)/shard_map/reduce_scatter | solution.py:119
  110.2 0.9 slice_maximum_fusion
  111.1 1.7 convolution_bitcast_fusion
  112.8 1.8 copy.13
  114.6 0.9 reshape.91
  115.6 25.2 %all_to_all.18 = f32[16,1,8192]{2,1,0:T(1,128)S(1)} all-to-all(f32[16,1,8192]{2,1,0:T(1,128)S(1)} %reshape.91), channel_id=1, replica_groups=mesh['frames'=16,'pix'=16] {'pix'}, dimensions={0} | all-to-all | bytes 1048576 | tf_op jit(solution)/shard_map/all_to_all | solution.py:122
  140.8 0.5 broadcast.106
  141.3 1.9 reduce
  143.2 0.7 reshape.92
  143.9 0.2 copy.15
  144.1 1.9 fusion.1
  146.0 1.9 fusion
  147.8 2.0 add_bitcast_fusion
  149.8 2.0 subtract_bitcast_fusion
  151.8 2.4 maximum_multiply_fusion
  154.2 5.5 %copy.18 = f32[256,2,8,256]{3,2,1,0:T(8,128)} copy(f32[256,2,8,256]{0,3,2,1:T(8,128)} %maximum_multiply_fusion) | data formatting | bytes 8388608 | tf_op jit(solution)/shard_map/mul | solution.py:133
  159.7 0.0 reduce-scatter.5.cloned.1.call-update
  159.7 78.4 %reduce-scatter.5.cloned.1.call-done = f32[16,2,8,256]{3,2,1,0:T(8,128)} async-done(((f32[256,2,8,256]{3,2,1,0:T(8,128)}), f32[16,2,8,256]{3,2,1,0:T(8,128)}) %reduce-scatter.5.cloned.1.call-update) | async-done | bytes 262160 | tf_op jit(solution)/shard_map/reduce_scatter | solution.py:132
  (1 shorter events, 0.0 us)
Async XLA Ops:
  6.5 103.7 %reduce-scatter.3.cloned.1.call-start = ((), (), s32[]{:S(2)}) async-start(), calls=%async_computation.3 | async-start | bytes 11141120 | tf_op jit(solution)/shard_map/reduce_scatter | solution.py:119
  6.5 2.2 copy-start
  8.7 0.9 copy-start.1
  9.7 0.9 copy-start.2
  10.6 0.9 copy-start.3
  11.6 0.7 copy-start.4
  34.1 204.1 %reduce-scatter.5.cloned.1.call-start = ((), (), s32[]{:S(2)}) async-start(), calls=%async_computation.4 | async-start | bytes 4456448 | tf_op jit(solution)/shard_map/reduce_scatter | solution.py:132
Sparse Core Ops, SparseCore 0:
  34.2 75.9 reduce-scatter.2
  159.9 78.2 reduce-scatter.4

commit v2 on v1

--- a/solution.py
+++ b/solution.py
@@ -2,6 +2,7 @@
 
 import jax
 import jax.numpy as jnp
+import numpy as np
 from jax import lax
 from jax.experimental import pallas as pl
 from jax.experimental.pallas import tpu as pltpu
@@ -13,9 +14,14 @@
 ROWS = 40
 TILE_BLOCK = 128
 GROUP = 16
-
-
-def bin_kernel(tiles_block, rows_ref, x_ref, chi_ref, split_ref, mask_ref, cake_ref, acc, vals, sem):
+MESH = pl.DeviceIdType.MESH
+SUBS = 8
+PARTS = 4
+TN = (((0,), (0,)), ((), ()))
+NT = (((1,), (1,)), ((), ()))
+
+
+def bin_kernel(tiles_block, rows_ref, x_ref, chi_ref, split_ref, mask_ref, cake_ref, count_ref, acc, vals, sem):
     step = pl.program_id(0)
     frames = x_ref.shape[0]
     bf = jnp.bfloat16
@@ -73,8 +79,15 @@
         for u in range(GROUP):
             q = rows_ref[(step + 1) * tiles_block - GROUP + u]
             acc[q] = acc[q] + vals[(groups - 1) % 2, u]
-        copy = pltpu.make_async_copy(acc, cake_ref, sem)
+        copy = pltpu.make_async_copy(acc.at[:, pl.ds(0, frames), :], cake_ref, sem)
         copy.start()
+
+        def rows_of(b, carry):
+            at = pl.ds(pl.multiple_of(b * 8, 8), 8)
+            count_ref[at, :] = acc[at, frames, :]
+            return carry
+
+        lax.fori_loop(0, NQ // 8, rows_of, 0)
         copy.wait()
 
 
@@ -85,12 +98,18 @@
     flat = pl.BlockSpec((block, 128), lambda i, rows: (i, 0))
     return pl.pallas_call(
         lambda *refs: bin_kernel(block, *refs),
-        out_shape=jax.ShapeDtypeStruct((NQ, ROWS, NCHI), jnp.float32),
+        out_shape=(
+            jax.ShapeDtypeStruct((NQ, frames, NCHI), jnp.float32),
+            jax.ShapeDtypeStruct((NQ, NCHI), jnp.float32),
+        ),
         grid_spec=pltpu.PrefetchScalarGridSpec(
             num_scalar_prefetch=1,
             grid=(tiles // block,),
             in_specs=[pl.BlockSpec((frames, block * 128), lambda i, rows: (0, i)), flat, flat, flat],
-            out_specs=pl.BlockSpec(memory_space=pl.ANY),
+            out_specs=(
+                pl.BlockSpec(memory_space=pl.ANY),
+                pl.BlockSpec((NQ, NCHI), lambda i, rows: (0, 0)),
+            ),
             scratch_shapes=[
                 pltpu.VMEM((NQ, ROWS, NCHI), jnp.float32),
                 pltpu.VMEM((2, GROUP, ROWS, NCHI), jnp.float32),
@@ -104,40 +123,387 @@
     )(tile_row, intensity, *(a.reshape(tiles, 128) for a in (chi_bin, split, mask)))
 
 
+def halves(x):
+    high = x.astype(jnp.bfloat16)
+    return high, (x - high.astype(jnp.float32)).astype(jnp.bfloat16)
+
+
+def dot(a, b, dims):
+    return lax.dot_general(a, b, dims, preferred_element_type=jnp.float32)
+
+
+def link_kernel(
+    chips, groups, cake_ref, count_ref, high_ref, low_ref, out_ref,
+    own, other, high_in, low_in, spectra, arrived, c1, c2, inverse,
+    sent, mine, theirs, corr, landed,
+    own_sem, pair_send, pair_recv, c1_send, c1_recv, c2_send, c2_recv,
+    ring_send, ring_recv, z_send, z_recv, swap_send, swap_recv, out_send, out_recv, self_sem,
+):
+    fg = lax.axis_index("frames")
+    p = lax.axis_index("pix")
+    z = p // 2
+    core = p % 2
+    devices = 2 * chips
+    frames = cake_ref.shape[1]
+    half = NQ // 2
+    part = half // PARTS
+    per = frames // SUBS
+    rows = 2 * NH // chips
+    lanes = per * half
+
+    def own_copy(i):
+        at = pl.ds(pl.multiple_of(i * part, 8), part)
+        src = pl.ds(pl.multiple_of(core * half + i * part, 8), part)
+        return pltpu.make_async_copy(cake_ref.at[src], own.at[at], own_sem.at[i])
+
+    for i in range(PARTS):
+        own_copy(i).start()
+
+    barrier = pltpu.get_barrier_semaphore()
+
+    def greet(d, carry):
+        pl.semaphore_signal(barrier, inc=1, device_id=(fg, (p + d) % devices), device_id_type=MESH)
+        return carry
+
+    def greet_frames(d, carry):
+        there = (fg + d) % groups
+        pl.semaphore_signal(barrier, inc=1, device_id=(there, p), device_id_type=MESH)
+        pl.semaphore_signal(barrier, inc=1, device_id=(there, 2 * z + 1 - core), device_id_type=MESH)
+        return carry
+
+    lax.fori_loop(1, devices, greet, 0)
+    lax.fori_loop(1, groups, greet_frames, 0)
+    pl.semaphore_wait(barrier, devices - 1 + 2 * (groups - 1))
+
+    def c1_copy(d):
+        to = (p + d) % devices
+        src = pl.ds(pl.multiple_of((to % 2) * half + fg * 8, 8), 8)
+        return pltpu.make_async_remote_copy(
+            src_ref=count_ref.at[src, :], dst_ref=c1.at[p], send_sem=c1_send.at[d], recv_sem=c1_recv.at[d],
+            device_id=(fg, to), device_id_type=MESH,
+        )
+
+    def c1_start(d, carry):
+        c1_copy(d).start()
+        return carry
+
+    lax.fori_loop(1, devices, c1_start, 0)
+
+    def pair_copy(i):
+        at = pl.ds(pl.multiple_of(i * part, 8), part)
+        src = pl.ds(pl.multiple_of((1 - core) * half + i * part, 8), part)
+        return pltpu.make_async_remote_copy(
+            src_ref=cake_ref.at[src], dst_ref=other.at[at], send_sem=pair_send.at[i], recv_sem=pair_recv.at[i],
+            device_id=(fg, 2 * z + 1 - core), device_id_type=MESH,
+        )
+
+    for i in range(PARTS):
+        pair_copy(i).start()
+
+    c1[p] = count_ref[pl.ds(pl.multiple_of(core * half + fg * 8, 8), 8), :]
+
+    def c1_wait(d, carry):
+        c1_copy(d).wait()
+        return carry
+
+    lax.fori_loop(1, devices, c1_wait, 0)
+    total = c1[0]
+    for i in range(1, devices):
+        total = total + c1[i]
+    here = pl.ds(pl.multiple_of(fg * 8, 8), 8)
+    c2[here, :] = total
+
+    def c2_copy(d):
+        return pltpu.make_async_remote_copy(
+            src_ref=c2.at[here, :], dst_ref=c2.at[here, :], send_sem=c2_send.at[d], recv_sem=c2_recv.at[d],
+            device_id=((fg + d) % groups, p), device_id_type=MESH,
+        )
+
+    def c2_landing(d):
+        at = pl.ds(pl.multiple_of((fg + groups - d) % groups * 8, 8), 8)
+        return pltpu.make_async_remote_copy(
+            src_ref=c2.at[here, :], dst_ref=c2.at[at, :], send_sem=c2_send.at[d], recv_sem=c2_recv.at[d],
+            device_id=((fg + d) % groups, p), device_id_type=MESH,
+        )
+
+    def c2_start(d, carry):
+        c2_copy(d).start()
+        return carry
+
+    def c2_wait(d, carry):
+        c2_copy(d).wait_send()
+        c2_landing(d).wait_recv()
+        return carry
+
+    lax.fori_loop(1, groups, c2_start, 0)
+    lax.fori_loop(1, groups, c2_wait, 0)
+    inverse[...] = 1.0 / jnp.maximum(c2[...], 1.0)
+
+    for i in range(PARTS):
+        own_copy(i).wait()
+        pair_copy(i).wait()
+
+    def normalise(n, carry):
+        b = n // (frames // 8)
+        f = n % (frames // 8)
+        qs = pl.ds(pl.multiple_of(b * 16, 16), 16)
+        fs = pl.ds(pl.multiple_of(f * 8, 8), 8)
+        both = jnp.swapaxes(own[qs, fs, :] + other[qs, fs, :], 0, 1) * inverse[qs, :][None]
+        h, l = halves(both)
+        high_in[fs, qs, :] = h
+        low_in[fs, qs, :] = l
+        return carry
+
+    lax.fori_loop(0, half // 16 * (frames // 8), normalise, 0)
+
+    def ring_copy(k, s):
+        sign = 1 - 2 * (k % 2)
+        block = (z - sign * (1 + s) + 2 * chips) % chips
+        at = pl.ds(pl.multiple_of(block * rows, 8), rows)
+        return pltpu.make_async_remote_copy(
+            src_ref=spectra.at[k, at, :], dst_ref=arrived.at[k, s],
+            send_sem=ring_send.at[k, s], recv_sem=ring_recv.at[k, s],
+            device_id=(fg, 2 * ((z + sign + chips) % chips) + core), device_id_type=MESH,
+        )
+
+    def transform(k, carry):
+        for t in range(0, per, 2):
+            fs = pl.ds(k * per + t, 2)
+            h = high_in[fs].reshape(2 * half, NCHI)
+            l = low_in[fs].reshape(2 * half, NCHI)
+            spectra[k, :, t * half:(t + 2) * half] = (
+                dot(high_ref[...], h, NT) + dot(high_ref[...], l, NT) + dot(low_ref[...], h, NT)
+            )
+        ring_copy(k, 0).start()
+        return carry
+
+    lax.fori_loop(0, SUBS, transform, 0)
+
+    def take(k, s):
+        sign = 1 - 2 * (k % 2)
+        block = (z - sign * (2 + s) + 2 * chips) % chips
+        at = pl.ds(pl.multiple_of(block * rows, 8), rows)
+        ring_copy(k, s).wait_recv()
+        spectra[k, at, :] = spectra[k, at, :] + arrived[k, s]
+
+    def ring_step(n, carry):
+        s = n // SUBS
+        k = n % SUBS
+        take(k, s)
+        ring_copy(k, s + 1).start()
+        return carry
+
+    lax.fori_loop(0, (chips - 2) * SUBS, ring_step, 0)
+
+    def z_copy(g, d):
+        to = (fg + d) % groups
+        fs = pl.ds(pl.multiple_of(g * 8, 8), 8)
+        return pltpu.make_async_remote_copy(
+            src_ref=sent.at[pl.ds(2 * to, 2), fs, :], dst_ref=mine.at[fg, :, fs, :],
+            send_sem=z_send.at[g, d], recv_sem=z_recv.at[g, d],
+            device_id=(to, p), device_id_type=MESH,
+        )
+
+    def z_landing(g, d):
+        fs = pl.ds(pl.multiple_of(g * 8, 8), 8)
+        return pltpu.make_async_remote_copy(
+            src_ref=sent.at[pl.ds(0, 2), fs, :], dst_ref=mine.at[(fg + groups - d) % groups, :, fs, :],
+            send_sem=z_send.at[g, d], recv_sem=z_recv.at[g, d],
+            device_id=((fg + d) % groups, p), device_id_type=MESH,
+        )
+
+    pack = 8 // per
+
+    def finish(g, carry):
+        for i in range(pack):
+            take(g * pack + i, chips - 2)
+        for t in range(rows // 8):
+            at = pl.ds(pl.multiple_of(z * rows + t * 8, 8), 8)
+            pieces = [
+                spectra[g * pack + i, at, f * half:(f + 1) * half] for i in range(pack) for f in range(per)
+            ]
+            turned = jnp.swapaxes(jnp.stack(pieces, 0), 0, 1)
+            sent[t * 8:t * 8 + 8, pl.ds(pl.multiple_of(g * 8, 8), 8), :] = turned
+
+        def z_start(d, carry):
+            z_copy(g, d).start()
+            return carry
+
+        lax.fori_loop(1, groups, z_start, 0)
+        return carry
+
+    lax.fori_loop(0, frames // 8, finish, 0)
+    mine[fg] = sent[pl.ds(2 * fg, 2)]
+
+    def z_wait(n, carry):
+        g = n // (groups - 1)
+        d = 1 + n % (groups - 1)
+        z_landing(g, d).wait_recv()
+        return carry
+
+    lax.fori_loop(0, frames // 8 * (groups - 1), z_wait, 0)
+
+    swap = pltpu.make_async_remote_copy(
+        src_ref=mine, dst_ref=theirs, send_sem=swap_send, recv_sem=swap_recv,
+        device_id=(fg, 2 * z + 1 - core), device_id_type=MESH,
+    )
+    swap.start()
+    total_frames = groups * frames
+    scale = 1.0 / math.sqrt(total_frames)
+
+    real = mine[:, 0].reshape(total_frames, half)
+    imag = mine[:, 1].reshape(total_frames, half)
+    real_high, real_low = halves(real)
+    imag_high, imag_low = halves(imag)
+
+    def left_of(r, i):
+        return jnp.concatenate([jnp.concatenate([r, i], 1), jnp.concatenate([i, -r], 1)], 0)
+
+    left_high = left_of(real_high, imag_high)
+    left_low = left_of(real_low, imag_low)
+
+    def product(right_high, right_low):
+        return (
+            dot(left_high, right_high, TN) + dot(left_high, right_low, TN) + dot(left_low, right_high, TN)
+        ) * scale
+
+    near = product(
+        jnp.concatenate([real_high, imag_high], 0), jnp.concatenate([real_low, imag_low], 0)
+    )
+    corr[core] = near.reshape(2, half, half)
+    swap.wait()
+    far_high, far_low = halves(
+        jnp.concatenate(
+            [theirs[:, 0].reshape(total_frames, half), theirs[:, 1].reshape(total_frames, half)], 0
+        )
+    )
+    corr[1 - core] = product(far_high, far_low).reshape(2, half, half)
+
+    block = NQ // groups
+    blocks = groups // 2
+    owner_core = fg // blocks
+
+    def out_copy(i):
+        return pltpu.make_async_remote_copy(
+            src_ref=corr.at[:, :, pl.ds(pl.multiple_of(i * block, 8), block), :], dst_ref=landed.at[fg % blocks],
+            send_sem=out_send.at[i], recv_sem=out_recv.at[fg % blocks],
+            device_id=(core * blocks + i, 2 * z + owner_core), device_id_type=MESH,
+        )
+
+    def out_landing(n):
+        return pltpu.make_async_remote_copy(
+            src_ref=corr.at[:, :, pl.ds(0, block), :], dst_ref=landed.at[n],
+            send_sem=out_send.at[n], recv_sem=out_recv.at[n],
+            device_id=(core * blocks + n, 2 * z + owner_core), device_id_type=MESH,
+        )
+
+    def out_start(i, carry):
+        @pl.when(core * blocks + i != fg)
+        def _():
+            out_copy(i).start()
+
+        return carry
+
+    lax.fori_loop(0, blocks, out_start, 0)
+
+    @pl.when(owner_core == core)
+    def _():
+        i = fg % blocks
+        keep = pltpu.make_async_copy(
+            corr.at[:, :, pl.ds(pl.multiple_of(i * block, 8), block), :], landed.at[i], self_sem
+        )
+        keep.start()
+        keep.wait()
+
+    def out_wait(n, carry):
+        @pl.when(core * blocks + n != fg)
+        def _():
+            out_landing(n).wait_recv()
+            out_copy(n).wait_send()
+
+        return carry
+
+    lax.fori_loop(0, blocks, out_wait, 0)
+    out_ref[...] = landed[...]
+
+    def ring_done(n, carry):
+        ring_copy(n % SUBS, n // SUBS).wait_send()
+        return carry
+
+    lax.fori_loop(0, (chips - 1) * SUBS, ring_done, 0)
+
+    def z_done(n, carry):
+        z_copy(n // (groups - 1), 1 + n % (groups - 1)).wait_send()
+        return carry
+
+    lax.fori_loop(0, frames // 8 * (groups - 1), z_done, 0)
+
+
+def linked(cake, counts, chips, groups):
+    frames = cake.shape[1]
+    devices = 2 * chips
+    half = NQ // 2
+    part = half // PARTS
+    per = frames // SUBS
+    rows = 2 * NH // chips
+    block = NQ // groups
+    blocks = groups // 2
+    high, low = fourier_table()
+    f32, bf = jnp.float32, jnp.bfloat16
+    dma = pltpu.SemaphoreType.DMA
+    vmem = pl.BlockSpec(memory_space=pltpu.VMEM)
+    return pl.pallas_call(
+        lambda *refs: link_kernel(chips, groups, *refs),
+        out_shape=jax.ShapeDtypeStruct((blocks, 2, 2, block, half), f32),
+        in_specs=[pl.BlockSpec(memory_space=pl.ANY), vmem, vmem, vmem],
+        out_specs=vmem,
+        scratch_shapes=[
+            pltpu.VMEM((half, frames, NCHI), f32),
+            pltpu.VMEM((half, frames, NCHI), f32),
+            pltpu.VMEM((frames, half, NCHI), bf),
+            pltpu.VMEM((frames, half, NCHI), bf),
+            pltpu.VMEM((SUBS, 2 * NH, per * half), f32),
+            pltpu.VMEM((SUBS, chips - 1, rows, per * half), f32),
+            pltpu.VMEM((devices, 8, NCHI), f32),
+            pltpu.VMEM((half, NCHI), f32),
+            pltpu.VMEM((half, NCHI), f32),
+            pltpu.VMEM((rows, frames, half), f32),
+            pltpu.VMEM((groups, 2, frames, half), f32),
+            pltpu.VMEM((groups, 2, frames, half), f32),
+            pltpu.VMEM((2, 2, half, half), f32),
+            pltpu.VMEM((blocks, 2, 2, block, half), f32),
+            dma((PARTS,)), dma((PARTS,)), dma((PARTS,)),
+            dma((devices,)), dma((devices,)), dma((groups,)), dma((groups,)),
+            dma((SUBS, chips - 1)), dma((SUBS, chips - 1)),
+            dma((frames // 8, groups)), dma((frames // 8, groups)),
+            dma(()), dma(()), dma((blocks,)), dma((blocks,)), dma(()),
+        ],
+        compiler_params=pltpu.CompilerParams(
+            collective_id=0, has_side_effects=True, vmem_limit_bytes=48 << 20
+        ),
+        name="links",
+    )(cake, counts, jnp.asarray(high), jnp.asarray(low))
+
+
 def fourier_table():
-    harmonic = lax.iota(jnp.int32, NH)[:, None]
-    column = lax.iota(jnp.int32, NCHI)[None, :]
-    phases = (harmonic * column % NCHI).astype(jnp.float32) * (2.0 * math.pi / NCHI)
-    factor = 1.0 / math.sqrt(NCHI)
-    return jnp.stack([jnp.cos(phases) * factor, -jnp.sin(phases) * factor], 0)
-
-
-def body(intensity, chi_bin, split, mask, tile_row):
-    frames_dev = intensity.shape[0]
-    high = lax.Precision.HIGHEST
-    cake = binned(intensity, chi_bin, split, mask, tile_row)[:, :frames_dev + 1]
-    block = lax.psum_scatter(cake, "pix", scatter_dimension=0, tiled=True)
-    normed = block[:, :frames_dev] / jnp.maximum(block[:, frames_dev:], 1.0)
-    local_spectra = jnp.einsum("qfc,rnc->frnq", normed, fourier_table(), precision=high)
-    spectra = lax.all_to_all(local_spectra, "pix", split_axis=2, concat_axis=3, tiled=True)
-    frame_scale = 1.0 / math.sqrt(frames_dev * lax.axis_size("frames"))
-    real_part = spectra[:, 0]
-    imag_part = spectra[:, 1]
-    real_corr = jnp.einsum("fnq,fnp->qnp", real_part, real_part, precision=high) + jnp.einsum(
-        "fnq,fnp->qnp", imag_part, imag_part, precision=high
-    )
-    imag_corr = jnp.einsum("fnq,fnp->qnp", imag_part, real_part, precision=high) - jnp.einsum(
-        "fnq,fnp->qnp", real_part, imag_part, precision=high
-    )
-    return lax.psum_scatter(
-        jnp.stack([real_corr, imag_corr], 1) * frame_scale,
-        "frames",
-        scatter_dimension=0,
-        tiled=True,
-    )
+    harmonic = np.arange(NH)[:, None]
+    phases = (harmonic * np.arange(NCHI)[None, :] % NCHI) * (2.0 * math.pi / NCHI)
+    table = np.stack([np.cos(phases), -np.sin(phases)], 1) / math.sqrt(NCHI)
+    table = table.reshape(2 * NH, NCHI).astype(np.float32)
+    high = table.astype(jnp.bfloat16)
+    return high, (table - high.astype(np.float32)).astype(jnp.bfloat16)
 
 
 def solution(mesh):
+    groups = mesh.shape["frames"]
+    chips = mesh.shape["pix"] // 2
+
+    def body(intensity, chi_bin, split, mask, tile_row):
+        cake, counts = binned(intensity, chi_bin, split, mask, tile_row)
+        blocks = linked(cake, counts, chips, groups)
+        n, h, c, q, r = blocks.shape
+        return blocks.transpose(3, 2, 0, 1, 4).reshape(q, c, n, h * r)
+
     in_specs = (P("frames", "pix"), P("pix"), P("pix"), P("pix"), P("pix"))
     out_specs = P("frames", None, "pix", None)
     return jax.shard_map(body, mesh=mesh, in_specs=in_specs, out_specs=out_specs, check_vma=False)

time: 246 us -> 114 us (0.46)
  waiting for transfers between devices: 154 us -> 0 us
  Pallas kernels: 21.8 us -> 102 us
  blocking collectives: 25.2 us -> 0 us
  between operations: 13.5 us -> 0.03 us
  matrix products: 9.33 us -> 0 us
  other arithmetic: 5.76 us -> 0 us
  local copies, waits for them, and re-layouts: 15.3 us -> 11.6 us
    reduce_scatter x2 -> x0, waiting for transfers between devices: 154 us -> none  [the longest x1 78.4 us: body(): lax.psum_scatter(jnp.stack([real_corr, imag_corr], 1) * frame_scale, 'fra...]
    pallas_call x1 -> x2, Pallas kernels: 21.8 us -> 102 us  [the longest x1 83.1 us: linked(): pl.pallas_call(lambda *refs: link_kernel(chips, groups, *refs), out_shape...]
    all_to_all x1 -> x0, blocking collectives: 25.2 us -> none  [body(): lax.all_to_all(local_spectra, 'pix', split_axis=2, concat_axis=3, tiled=T...]
    dot_general x5 -> x0, matrix products: 9.33 us -> none  [the longest x1 1.99 us: body(): jnp.einsum('fnq,fnp->qnp', real_part, imag_part, precision=high)]
    mul x1 -> x0, local copies, waits for them, and re-layouts: 5.48 us -> none  [body(): jnp.stack([real_corr, imag_corr], 1) * frame_scale]
    unnamed x13 -> x16, local copies, waits for them, and re-layouts: 7.32 us -> 10.7 us
    mul x2 -> x0, other arithmetic: 2.96 us -> none  [the longest x1 2.42 us: body(): jnp.stack([real_corr, imag_corr], 1) * frame_scale]
  transfers between devices with their start and end apart: 2 -> 0, of which waited for: 2 -> 0; matrix products, arithmetic and copies ran while one was open for 0% -> 0% of each run, Pallas kernels for 0% -> 0%
where the time goes in v2:
time: 114 us
  Pallas kernels  102 us (89%)
  local copies, waits for them, and re-layouts  11.6 us (10%)
    pallas_call x1, Pallas kernels, linked(): pl.pallas_call(lambda *refs: link_kernel(chips, groups, *refs), out_shape...  83.1 us
    pallas_call x1, Pallas kernels, binned(): pl.pallas_call(lambda *refs: bin_kernel(block, *refs), out_shape=(jax.Sha...  19.2 us
    unnamed x16, local copies, waits for them, and re-layouts  10.7 us

profile of v2, /device:TPU:1, one launch (start us, length us, event | category | flops | bytes accessed | tf_op | source)
XLA Modules:
  0.0 113.9 jit_solution(16581205985583086067)
XLA Ops:
  0.0 0.0 copy-start.1
  0.0 2.2 %copy-done.1 = bf16[32,65536]{1,0:T(8,128)(2,1)S(1)} copy-done((bf16[32,65536]{1,0:T(8,128)(2,1)S(1)}, bf16[32,65536]{1,0:T(8,128)(2,1)}, u32[]{:S(2)}) %copy-start.1) | copy-done | bytes 4194328
  2.2 0.0 copy-start.2
  2.2 0.9 copy-done.2
  3.1 0.0 copy-start.3
  3.1 0.9 copy-done.3
  4.1 0.0 copy-start.4
  4.1 0.9 copy-done.4
  5.0 0.0 copy-start.7
  5.0 0.7 copy-done.7
  5.7 19.2 %binning.1 = (f32[256,32,256]{2,1,0:T(8,128)S(1)}, f32[256,256]{1,0:T(8,128)S(1)}) custom-call(s32[512]{0:T(512)S(1)} %copy-done.7, bf16[32,65536]{1,0:T(8,128)(2,1)S(1)} %copy-done.1, s32[512,128]{1,0:T(8,128)S(1)} %bitcast.8, f32[512,128]{1,0:T(8,128)S(1)} %bitcast.9, s32[512,128]{1,0:T(8,128)S(1)} %bitcast.10), custom_call_target="tpu_custom_call" | custom-call | tf_op jit(solution)/shard_map/binning/pallas_call | solution.py:99
  24.9 0.0 copy-start
  24.9 3.2 %copy-done = f32[256,32,256]{2,1,0:T(8,128)} copy-done((f32[256,32,256]{2,1,0:T(8,128)}, f32[256,32,256]{2,1,0:T(8,128)S(1)}, u32[]{:S(2)}) %copy-start) | copy-done | bytes 8388632
  28.2 0.0 copy-start.5
  28.2 0.9 copy-done.5
  29.1 0.0 copy-start.6
  29.1 0.9 copy-done.6
  30.0 83.1 %links.1 = f32[8,2,2,16,128]{4,3,2,1,0:T(8,128)S(1)} custom-call(f32[256,32,256]{2,1,0:T(8,128)} %copy-done, f32[256,256]{1,0:T(8,128)S(1)} %get-tuple-element.8.refs_1_, bf16[256,256]{1,0:T(8,128)(2,1)S(1)} %copy-done.6, bf16[256,256]{1,0:T(8,128)(2,1)S(1)} %copy-done.5), custom_call_target="tpu_custom_call" | custom-call | tf_op jit(solution)/shard_map/links/pallas_call | solution.py:455
  113.1 0.9 copy.10
Async XLA Ops:
  0.0 2.2 %copy-start.1 = (bf16[32,65536]{1,0:T(8,128)(2,1)S(1)}, bf16[32,65536]{1,0:T(8,128)(2,1)}, u32[]{:S(2)}) copy-start(bf16[32,65536]{1,0:T(8,128)(2,1)} %refs_1_.1) | copy-start | bytes 12582916
  2.2 0.9 copy-start.2
  3.1 0.9 copy-start.3
  4.1 0.9 copy-start.4
  5.0 0.7 copy-start.7
  24.9 3.2 %copy-start = (f32[256,32,256]{2,1,0:T(8,128)}, f32[256,32,256]{2,1,0:T(8,128)S(1)}, u32[]{:S(2)}) copy-start(f32[256,32,256]{2,1,0:T(8,128)S(1)} %get-tuple-element.7.refs_0_) | copy-start | bytes 25165828
  28.2 0.9 copy-start.5
  29.1 0.9 copy-start.6

commit v3 on v2

--- a/solution.py
+++ b/solution.py
@@ -12,8 +12,10 @@
 NCHI = 256
 NH = 128
 ROWS = 40
-TILE_BLOCK = 128
+TILE_BLOCK = 64
 GROUP = 16
+BIN_VMEM = 36 << 20
+LINK_VMEM = 36 << 20
 MESH = pl.DeviceIdType.MESH
 SUBS = 8
 PARTS = 4
@@ -21,15 +23,36 @@
 NT = (((1,), (1,)), ((), ()))
 
 
-def bin_kernel(tiles_block, rows_ref, x_ref, chi_ref, split_ref, mask_ref, cake_ref, count_ref, acc, vals, sem):
-    step = pl.program_id(0)
+def bin_kernel(
+    rows_any, x_any, chi_any, split_any, mask_any, cake_ref, count_ref,
+    rows_ref, x_ref, chi_ref, split_ref, mask_ref, count_acc, vals, rows_sem, sem,
+):
     frames = x_ref.shape[0]
+    tiles = chi_ref.shape[0]
+    blocks = tiles // TILE_BLOCK
     bf = jnp.bfloat16
 
-    @pl.when(step == 0)
-    def _():
-        acc[...] = jnp.zeros_like(acc)
-        vals[...] = jnp.zeros_like(vals)
+    def copies(b):
+        at = pl.ds(pl.multiple_of(b * TILE_BLOCK, 8), TILE_BLOCK)
+        wide = pl.ds(pl.multiple_of(b * TILE_BLOCK * 128, 128), TILE_BLOCK * 128)
+        pairs = ((chi_any, chi_ref), (split_any, split_ref), (mask_any, mask_ref))
+        flat = [pltpu.make_async_copy(a.at[at, :], r.at[at, :], sem.at[b, n]) for n, (a, r) in enumerate(pairs)]
+        return flat + [pltpu.make_async_copy(x_any.at[:, wide], x_ref.at[:, wide], sem.at[b, 3])]
+
+    rows_copy = pltpu.make_async_copy(rows_any, rows_ref, rows_sem)
+    rows_copy.start()
+    for b in range(blocks):
+        for copy in copies(b):
+            copy.start()
+
+    def clear(n, carry):
+        at = pl.ds(n * 8, 8)
+        cake_ref[at] = jnp.zeros((8, frames, NCHI), jnp.float32)
+        count_acc[at] = jnp.zeros((8, 8, NCHI), jnp.float32)
+        return carry
+
+    lax.fori_loop(0, NQ // 8, clear, 0)
+    vals[...] = jnp.zeros_like(vals)
 
     zero = jnp.zeros((), bf)
     columns = lax.broadcasted_iota(jnp.int32, (NCHI, 128), 0).astype(jnp.float32).astype(bf)
@@ -48,8 +71,20 @@
         after = ((chi + 1) & (NCHI - 1)).astype(jnp.float32).astype(bf)
         return jnp.where(columns == here, near, jnp.where(columns == after, far, zero))
 
+    def add(first, slot):
+        for u in range(GROUP):
+            q = rows_ref[first + u]
+            cake_ref[q] = cake_ref[q] + vals[slot, u, :frames]
+            count_acc[q] = count_acc[q] + vals[slot, u, frames:]
+
     def group(g, carry):
         slot = lax.rem(g, 2)
+
+        @pl.when(lax.rem(g * GROUP, TILE_BLOCK) == 0)
+        def _():
+            for copy in copies(g * GROUP // TILE_BLOCK):
+                copy.wait()
+
         for u in range(0, GROUP, 2):
             t = g * GROUP + u
             weights = jnp.concatenate([weights_of(t), weights_of(t + 1)], axis=1)
@@ -58,69 +93,58 @@
             left = jnp.concatenate(
                 [jnp.concatenate([a, blank], 1), jnp.concatenate([blank, b], 1), ones], axis=0
             )
-            value = lax.dot_general(
-                left, weights, (((1,), (1,)), ((), ())), preferred_element_type=jnp.float32
-            )
+            value = dot(left, weights, NT)
             vals[slot, u, :frames] = value[:frames]
             vals[slot, u, frames:] = value[2 * frames:2 * frames + 8]
             vals[slot, u + 1, :frames] = value[frames:2 * frames]
             vals[slot, u + 1, frames:] = value[2 * frames + 8:]
-        before = jnp.maximum(step * tiles_block + (g - 1) * GROUP, 0)
-        for u in range(GROUP):
-            q = rows_ref[before + u]
-            acc[q] = acc[q] + vals[1 - slot, u]
-        return carry
-
-    groups = tiles_block // GROUP
+        add(jnp.maximum((g - 1) * GROUP, 0), 1 - slot)
+        return carry
+
+    rows_copy.wait()
+    groups = tiles // GROUP
     lax.fori_loop(0, groups, group, 0)
-
-    @pl.when(step == pl.num_programs(0) - 1)
-    def _():
-        for u in range(GROUP):
-            q = rows_ref[(step + 1) * tiles_block - GROUP + u]
-            acc[q] = acc[q] + vals[(groups - 1) % 2, u]
-        copy = pltpu.make_async_copy(acc.at[:, pl.ds(0, frames), :], cake_ref, sem)
-        copy.start()
-
-        def rows_of(b, carry):
-            at = pl.ds(pl.multiple_of(b * 8, 8), 8)
-            count_ref[at, :] = acc[at, frames, :]
-            return carry
-
-        lax.fori_loop(0, NQ // 8, rows_of, 0)
-        copy.wait()
+    add(tiles - GROUP, (groups - 1) % 2)
+
+    def rows_of(b, carry):
+        at = pl.ds(pl.multiple_of(b * 8, 8), 8)
+        count_ref[at, :] = count_acc[at, 0, :]
+        return carry
+
+    lax.fori_loop(0, NQ // 8, rows_of, 0)
+
+
+def stay(a):
+    return pltpu.with_memory_space_constraint(a, pltpu.HBM)
 
 
 def binned(intensity, chi_bin, split, mask, tile_row):
-    frames = intensity.shape[0]
+    frames, pixels = intensity.shape
     tiles = tile_row.shape[0]
-    block = TILE_BLOCK
-    flat = pl.BlockSpec((block, 128), lambda i, rows: (i, 0))
+    vmem = pl.BlockSpec(memory_space=pltpu.VMEM)
+    away = pl.BlockSpec(memory_space=pltpu.HBM)
     return pl.pallas_call(
-        lambda *refs: bin_kernel(block, *refs),
+        bin_kernel,
         out_shape=(
             jax.ShapeDtypeStruct((NQ, frames, NCHI), jnp.float32),
             jax.ShapeDtypeStruct((NQ, NCHI), jnp.float32),
         ),
-        grid_spec=pltpu.PrefetchScalarGridSpec(
-            num_scalar_prefetch=1,
-            grid=(tiles // block,),
-            in_specs=[pl.BlockSpec((frames, block * 128), lambda i, rows: (0, i)), flat, flat, flat],
-            out_specs=(
-                pl.BlockSpec(memory_space=pl.ANY),
-                pl.BlockSpec((NQ, NCHI), lambda i, rows: (0, 0)),
-            ),
-            scratch_shapes=[
-                pltpu.VMEM((NQ, ROWS, NCHI), jnp.float32),
-                pltpu.VMEM((2, GROUP, ROWS, NCHI), jnp.float32),
-                pltpu.SemaphoreType.DMA,
-            ],
-        ),
-        compiler_params=pltpu.CompilerParams(
-            dimension_semantics=("arbitrary",), vmem_limit_bytes=40 << 20
-        ),
+        in_specs=[away, away, away, away, away],
+        out_specs=(vmem, vmem),
+        scratch_shapes=[
+            pltpu.SMEM((tiles,), jnp.int32),
+            pltpu.VMEM((frames, pixels), jnp.bfloat16),
+            pltpu.VMEM((tiles, 128), jnp.int32),
+            pltpu.VMEM((tiles, 128), jnp.float32),
+            pltpu.VMEM((tiles, 128), jnp.int32),
+            pltpu.VMEM((NQ, 8, NCHI), jnp.float32),
+            pltpu.VMEM((2, GROUP, ROWS, NCHI), jnp.float32),
+            pltpu.SemaphoreType.DMA,
+            pltpu.SemaphoreType.DMA((tiles // TILE_BLOCK, 4)),
+        ],
+        compiler_params=pltpu.CompilerParams(vmem_limit_bytes=BIN_VMEM),
         name="binning",
-    )(tile_row, intensity, *(a.reshape(tiles, 128) for a in (chi_bin, split, mask)))
+    )(*(stay(a) for a in (tile_row, intensity, *(a.reshape(tiles, 128) for a in (chi_bin, split, mask)))))
 
 
 def halves(x):
@@ -133,10 +157,10 @@
 
 
 def link_kernel(
-    chips, groups, cake_ref, count_ref, high_ref, low_ref, out_ref,
-    own, other, high_in, low_in, spectra, arrived, c1, c2, inverse,
+    chips, groups, cake_ref, count_ref, high_any, low_any, out_ref,
+    high_ref, low_ref, other, high_in, low_in, spectra, arrived, c1, c2, inverse,
     sent, mine, theirs, corr, landed,
-    own_sem, pair_send, pair_recv, c1_send, c1_recv, c2_send, c2_recv,
+    table_sem, pair_send, pair_recv, c1_send, c1_recv, c2_send, c2_recv,
     ring_send, ring_recv, z_send, z_recv, swap_send, swap_recv, out_send, out_recv, self_sem,
 ):
     fg = lax.axis_index("frames")
@@ -151,13 +175,12 @@
     rows = 2 * NH // chips
     lanes = per * half
 
-    def own_copy(i):
-        at = pl.ds(pl.multiple_of(i * part, 8), part)
-        src = pl.ds(pl.multiple_of(core * half + i * part, 8), part)
-        return pltpu.make_async_copy(cake_ref.at[src], own.at[at], own_sem.at[i])
-
-    for i in range(PARTS):
-        own_copy(i).start()
+    tables = [
+        pltpu.make_async_copy(high_any, high_ref, table_sem.at[0]),
+        pltpu.make_async_copy(low_any, low_ref, table_sem.at[1]),
+    ]
+    for copy in tables:
+        copy.start()
 
     barrier = pltpu.get_barrier_semaphore()
 
@@ -239,22 +262,10 @@
     lax.fori_loop(1, groups, c2_wait, 0)
     inverse[...] = 1.0 / jnp.maximum(c2[...], 1.0)
 
+    for copy in tables:
+        copy.wait()
     for i in range(PARTS):
-        own_copy(i).wait()
         pair_copy(i).wait()
-
-    def normalise(n, carry):
-        b = n // (frames // 8)
-        f = n % (frames // 8)
-        qs = pl.ds(pl.multiple_of(b * 16, 16), 16)
-        fs = pl.ds(pl.multiple_of(f * 8, 8), 8)
-        both = jnp.swapaxes(own[qs, fs, :] + other[qs, fs, :], 0, 1) * inverse[qs, :][None]
-        h, l = halves(both)
-        high_in[fs, qs, :] = h
-        low_in[fs, qs, :] = l
-        return carry
-
-    lax.fori_loop(0, half // 16 * (frames // 8), normalise, 0)
 
     def ring_copy(k, s):
         sign = 1 - 2 * (k % 2)
@@ -266,18 +277,32 @@
             device_id=(fg, 2 * ((z + sign + chips) % chips) + core), device_id_type=MESH,
         )
 
-    def transform(k, carry):
-        for t in range(0, per, 2):
-            fs = pl.ds(k * per + t, 2)
-            h = high_in[fs].reshape(2 * half, NCHI)
-            l = low_in[fs].reshape(2 * half, NCHI)
-            spectra[k, :, t * half:(t + 2) * half] = (
-                dot(high_ref[...], h, NT) + dot(high_ref[...], l, NT) + dot(low_ref[...], h, NT)
-            )
-        ring_copy(k, 0).start()
-        return carry
-
-    lax.fori_loop(0, SUBS, transform, 0)
+    def transform(g, carry):
+        fs = pl.ds(pl.multiple_of(g * 8, 8), 8)
+
+        def normalise(b, carry):
+            qs = pl.ds(pl.multiple_of(b * 16, 16), 16)
+            mine_qs = pl.ds(pl.multiple_of(core * half + b * 16, 16), 16)
+            both = jnp.swapaxes(cake_ref[mine_qs, fs, :] + other[qs, fs, :], 0, 1) * inverse[qs, :][None]
+            h, l = halves(both)
+            high_in[:, qs, :] = h
+            low_in[:, qs, :] = l
+            return carry
+
+        lax.fori_loop(0, half // 16, normalise, 0)
+        for i in range(8 // per):
+            k = g * (8 // per) + i
+            for t in range(0, per, 2):
+                pick = slice(i * per + t, i * per + t + 2)
+                h = high_in[pick].reshape(2 * half, NCHI)
+                l = low_in[pick].reshape(2 * half, NCHI)
+                spectra[k, :, t * half:(t + 2) * half] = (
+                    dot(high_ref[...], h, NT) + dot(high_ref[...], l, NT) + dot(low_ref[...], h, NT)
+                )
+            ring_copy(k, 0).start()
+        return carry
+
+    lax.fori_loop(0, frames // 8, transform, 0)
 
     def take(k, s):
         sign = 1 - 2 * (k % 2)
@@ -330,54 +355,62 @@
             return carry
 
         lax.fori_loop(1, groups, z_start, 0)
+        fs = pl.ds(pl.multiple_of(g * 8, 8), 8)
+        mine[fg, :, fs, :] = sent[pl.ds(2 * fg, 2), fs, :]
         return carry
 
     lax.fori_loop(0, frames // 8, finish, 0)
-    mine[fg] = sent[pl.ds(2 * fg, 2)]
-
-    def z_wait(n, carry):
-        g = n // (groups - 1)
-        d = 1 + n % (groups - 1)
-        z_landing(g, d).wait_recv()
-        return carry
-
-    lax.fori_loop(0, frames // 8 * (groups - 1), z_wait, 0)
-
-    swap = pltpu.make_async_remote_copy(
-        src_ref=mine, dst_ref=theirs, send_sem=swap_send, recv_sem=swap_recv,
-        device_id=(fg, 2 * z + 1 - core), device_id_type=MESH,
-    )
-    swap.start()
-    total_frames = groups * frames
-    scale = 1.0 / math.sqrt(total_frames)
-
-    real = mine[:, 0].reshape(total_frames, half)
-    imag = mine[:, 1].reshape(total_frames, half)
-    real_high, real_low = halves(real)
-    imag_high, imag_low = halves(imag)
-
-    def left_of(r, i):
-        return jnp.concatenate([jnp.concatenate([r, i], 1), jnp.concatenate([i, -r], 1)], 0)
-
-    left_high = left_of(real_high, imag_high)
-    left_low = left_of(real_low, imag_low)
-
-    def product(right_high, right_low):
+
+    def swap_copy(g):
+        fs = pl.ds(pl.multiple_of(g * 8, 8), 8)
+        return pltpu.make_async_remote_copy(
+            src_ref=mine.at[:, :, fs, :], dst_ref=theirs.at[:, :, fs, :],
+            send_sem=swap_send.at[g], recv_sem=swap_recv.at[g],
+            device_id=(fg, 2 * z + 1 - core), device_id_type=MESH,
+        )
+
+    scale = 1.0 / math.sqrt(groups * frames)
+
+    def pieces_of(ref, g):
+        fs = pl.ds(pl.multiple_of(g * 8, 8), 8)
+        real = halves(ref[:, 0, fs, :].reshape(groups * 8, half))
+        imag = halves(ref[:, 1, fs, :].reshape(groups * 8, half))
+        return real, imag
+
+    def product(g, ref):
+        real, imag = pieces_of(mine, g)
+        left = [
+            jnp.concatenate([jnp.concatenate([r, i], 1), jnp.concatenate([i, -r], 1)], 0)
+            for r, i in zip(real, imag)
+        ]
+        right = [jnp.concatenate([r, i], 0) for r, i in zip(*pieces_of(ref, g))]
         return (
-            dot(left_high, right_high, TN) + dot(left_high, right_low, TN) + dot(left_low, right_high, TN)
-        ) * scale
-
-    near = product(
-        jnp.concatenate([real_high, imag_high], 0), jnp.concatenate([real_low, imag_low], 0)
-    )
-    corr[core] = near.reshape(2, half, half)
-    swap.wait()
-    far_high, far_low = halves(
-        jnp.concatenate(
-            [theirs[:, 0].reshape(total_frames, half), theirs[:, 1].reshape(total_frames, half)], 0
-        )
-    )
-    corr[1 - core] = product(far_high, far_low).reshape(2, half, half)
+            (dot(left[0], right[0], TN) + dot(left[0], right[1], TN) + dot(left[1], right[0], TN)) * scale
+        ).reshape(2, half, half)
+
+    corr[...] = jnp.zeros_like(corr)
+
+    def other_half(g):
+        swap_copy(g).wait_recv()
+        corr[1 - core] = corr[1 - core] + product(g, theirs)
+
+    def correlate(g, carry):
+        def z_wait(d, carry):
+            z_landing(g, d).wait_recv()
+            return carry
+
+        lax.fori_loop(1, groups, z_wait, 0)
+        swap_copy(g).start()
+        corr[core] = corr[core] + product(g, mine)
+
+        @pl.when(g > 0)
+        def _():
+            other_half(g - 1)
+
+        return carry
+
+    lax.fori_loop(0, frames // 8, correlate, 0)
+    other_half(frames // 8 - 1)
 
     block = NQ // groups
     blocks = groups // 2
@@ -425,6 +458,9 @@
 
     lax.fori_loop(0, blocks, out_wait, 0)
     out_ref[...] = landed[...]
+
+    for g in range(frames // 8):
+        swap_copy(g).wait_send()
 
     def ring_done(n, carry):
         ring_copy(n % SUBS, n // SUBS).wait_send()
@@ -451,17 +487,19 @@
     high, low = fourier_table()
     f32, bf = jnp.float32, jnp.bfloat16
     dma = pltpu.SemaphoreType.DMA
+    away = pl.BlockSpec(memory_space=pltpu.HBM)
     vmem = pl.BlockSpec(memory_space=pltpu.VMEM)
     return pl.pallas_call(
         lambda *refs: link_kernel(chips, groups, *refs),
         out_shape=jax.ShapeDtypeStruct((blocks, 2, 2, block, half), f32),
-        in_specs=[pl.BlockSpec(memory_space=pl.ANY), vmem, vmem, vmem],
+        in_specs=[vmem, vmem, away, away],
         out_specs=vmem,
         scratch_shapes=[
+            pltpu.VMEM((2 * NH, NCHI), bf),
+            pltpu.VMEM((2 * NH, NCHI), bf),
             pltpu.VMEM((half, frames, NCHI), f32),
-            pltpu.VMEM((half, frames, NCHI), f32),
-            pltpu.VMEM((frames, half, NCHI), bf),
-            pltpu.VMEM((frames, half, NCHI), bf),
+            pltpu.VMEM((8, half, NCHI), bf),
+            pltpu.VMEM((8, half, NCHI), bf),
             pltpu.VMEM((SUBS, 2 * NH, per * half), f32),
             pltpu.VMEM((SUBS, chips - 1, rows, per * half), f32),
             pltpu.VMEM((devices, 8, NCHI), f32),
@@ -472,17 +510,17 @@
             pltpu.VMEM((groups, 2, frames, half), f32),
             pltpu.VMEM((2, 2, half, half), f32),
             pltpu.VMEM((blocks, 2, 2, block, half), f32),
-            dma((PARTS,)), dma((PARTS,)), dma((PARTS,)),
+            dma((2,)), dma((PARTS,)), dma((PARTS,)),
             dma((devices,)), dma((devices,)), dma((groups,)), dma((groups,)),
             dma((SUBS, chips - 1)), dma((SUBS, chips - 1)),
             dma((frames // 8, groups)), dma((frames // 8, groups)),
-            dma(()), dma(()), dma((blocks,)), dma((blocks,)), dma(()),
+            dma((frames // 8,)), dma((frames // 8,)), dma((blocks,)), dma((blocks,)), dma(()),
         ],
         compiler_params=pltpu.CompilerParams(
-            collective_id=0, has_side_effects=True, vmem_limit_bytes=48 << 20
+            collective_id=0, has_side_effects=True, vmem_limit_bytes=LINK_VMEM
         ),
         name="links",
-    )(cake, counts, jnp.asarray(high), jnp.asarray(low))
+    )(cake, counts, stay(jnp.asarray(high)), stay(jnp.asarray(low)))
 
 
 def fourier_table():

time: 114 us -> 101 us (0.89)
  local copies, waits for them, and re-layouts: 11.6 us -> 0.86 us
  Pallas kernels: 102 us -> 99.8 us
    unnamed x16 -> x0, local copies, waits for them, and re-layouts: 10.7 us -> none
    pallas_call x1, Pallas kernels: 83.1 us -> 81.1 us  [linked(): pl.pallas_call(lambda *refs: link_kernel(chips, groups, *refs), out_shape...]
where the time goes in v3:
time: 101 us
  Pallas kernels  99.8 us (99%)
    pallas_call x1, Pallas kernels, linked(): pl.pallas_call(lambda *refs: link_kernel(chips, groups, *refs), out_shape...  81.1 us
    pallas_call x1, Pallas kernels, binned(): pl.pallas_call(bin_kernel, out_shape=(jax.ShapeDtypeStruct((NQ, frames, N...  18.7 us

profile of v3, /device:TPU:1, one launch (start us, length us, event | category | flops | bytes accessed | tf_op | source)
XLA Modules:
  0.0 100.7 jit_solution(17913580236106539561)
XLA Ops:
  0.0 18.7 %binning.1 = (f32[256,32,256]{2,1,0:T(8,128)S(1)}, f32[256,256]{1,0:T(8,128)S(1)}) custom-call(s32[512]{0:T(512)} %rows_any.1, bf16[32,65536]{1,0:T(8,128)(2,1)} %x_any.1, s32[512,128]{1,0:T(8,128)} %bitcast.8, f32[512,128]{1,0:T(8,128)} %bitcast.9, s32[512,128]{1,0:T(8,128)} %bitcast.10), custom_call_target="tpu_custom_call" | custom-call | tf_op jit(solution)/shard_map/binning/pallas_call | solution.py:126
  18.8 81.1 %links.1 = f32[8,2,2,16,128]{4,3,2,1,0:T(8,128)S(1)} custom-call(f32[256,32,256]{2,1,0:T(8,128)S(1)} %get-tuple-element.7.refs_0_, f32[256,256]{1,0:T(8,128)S(1)} %get-tuple-element.8.refs_1_, bf16[256,256]{1,0:T(8,128)(2,1)} %constant.4.clone.refs_2_, bf16[256,256]{1,0:T(8,128)(2,1)} %constant.5.clone.refs_3_), custom_call_target="tpu_custom_call" | custom-call | tf_op jit(solution)/shard_map/links/pallas_call | solution.py:492
  99.8 0.9 copy.10

commit v4 on v3

--- a/solution.py
+++ b/solution.py
@@ -13,11 +13,12 @@
 NH = 128
 ROWS = 40
 TILE_BLOCK = 64
-GROUP = 16
+GROUP = 32
 BIN_VMEM = 36 << 20
 LINK_VMEM = 36 << 20
 MESH = pl.DeviceIdType.MESH
 SUBS = 8
+UNROLL = 5
 PARTS = 4
 TN = (((0,), (0,)), ((), ()))
 NT = (((1,), (1,)), ((), ()))
@@ -158,7 +159,7 @@
 
 def link_kernel(
     chips, groups, cake_ref, count_ref, high_any, low_any, out_ref,
-    high_ref, low_ref, other, high_in, low_in, spectra, arrived, c1, c2, inverse,
+    high_ref, low_ref, other, raw, spectra, arrived, c1, c2, inverse,
     sent, mine, theirs, corr, landed,
     table_sem, pair_send, pair_recv, c1_send, c1_recv, c2_send, c2_recv,
     ring_send, ring_recv, z_send, z_recv, swap_send, swap_recv, out_send, out_recv, self_sem,
@@ -189,14 +190,23 @@
         return carry
 
     def greet_frames(d, carry):
-        there = (fg + d) % groups
-        pl.semaphore_signal(barrier, inc=1, device_id=(there, p), device_id_type=MESH)
-        pl.semaphore_signal(barrier, inc=1, device_id=(there, 2 * z + 1 - core), device_id_type=MESH)
-        return carry
-
-    lax.fori_loop(1, devices, greet, 0)
-    lax.fori_loop(1, groups, greet_frames, 0)
-    pl.semaphore_wait(barrier, devices - 1 + 2 * (groups - 1))
+        pl.semaphore_signal(barrier, inc=1, device_id=((fg + d) % groups, p), device_id_type=MESH)
+        return carry
+
+    def greet_owners(i, carry):
+        to = core * (groups // 2) + i
+        pl.semaphore_signal(barrier, inc=1, device_id=(to, 2 * z + 1 - core), device_id_type=MESH)
+        return carry
+
+    lax.fori_loop(1, devices, greet, 0, unroll=UNROLL)
+    lax.fori_loop(1, groups, greet_frames, 0, unroll=UNROLL)
+
+    @pl.when(fg // (groups // 2) != core)
+    def _():
+        lax.fori_loop(0, groups // 2, greet_owners, 0, unroll=UNROLL)
+
+    apart = fg // (groups // 2) - core
+    pl.semaphore_wait(barrier, devices + groups - 2 + groups // 2 * apart * apart)
 
     def c1_copy(d):
         to = (p + d) % devices
@@ -210,7 +220,7 @@
         c1_copy(d).start()
         return carry
 
-    lax.fori_loop(1, devices, c1_start, 0)
+    lax.fori_loop(1, devices, c1_start, 0, unroll=UNROLL)
 
     def pair_copy(i):
         at = pl.ds(pl.multiple_of(i * part, 8), part)
@@ -229,7 +239,7 @@
         c1_copy(d).wait()
         return carry
 
-    lax.fori_loop(1, devices, c1_wait, 0)
+    lax.fori_loop(1, devices, c1_wait, 0, unroll=UNROLL)
     total = c1[0]
     for i in range(1, devices):
         total = total + c1[i]
@@ -258,15 +268,25 @@
         c2_landing(d).wait_recv()
         return carry
 
-    lax.fori_loop(1, groups, c2_start, 0)
-    lax.fori_loop(1, groups, c2_wait, 0)
-    inverse[...] = 1.0 / jnp.maximum(c2[...], 1.0)
+    lax.fori_loop(1, groups, c2_start, 0, unroll=UNROLL)
 
     for copy in tables:
         copy.wait()
     for i in range(PARTS):
         pair_copy(i).wait()
 
+    def gather(n, carry):
+        b = n // (frames // 8)
+        qs = pl.ds(pl.multiple_of(b * 16, 16), 16)
+        mine_qs = pl.ds(pl.multiple_of(core * half + b * 16, 16), 16)
+        fs = pl.ds(pl.multiple_of(n % (frames // 8) * 8, 8), 8)
+        raw[fs, qs, :] = jnp.swapaxes(cake_ref[mine_qs, fs, :] + other[qs, fs, :], 0, 1)
+        return carry
+
+    lax.fori_loop(0, half // 16 * (frames // 8), gather, 0)
+    lax.fori_loop(1, groups, c2_wait, 0, unroll=UNROLL)
+    inverse[...] = 1.0 / jnp.maximum(c2[...], 1.0)
+
     def ring_copy(k, s):
         sign = 1 - 2 * (k % 2)
         block = (z - sign * (1 + s) + 2 * chips) % chips
@@ -277,32 +297,17 @@
             device_id=(fg, 2 * ((z + sign + chips) % chips) + core), device_id_type=MESH,
         )
 
-    def transform(g, carry):
-        fs = pl.ds(pl.multiple_of(g * 8, 8), 8)
-
-        def normalise(b, carry):
-            qs = pl.ds(pl.multiple_of(b * 16, 16), 16)
-            mine_qs = pl.ds(pl.multiple_of(core * half + b * 16, 16), 16)
-            both = jnp.swapaxes(cake_ref[mine_qs, fs, :] + other[qs, fs, :], 0, 1) * inverse[qs, :][None]
-            h, l = halves(both)
-            high_in[:, qs, :] = h
-            low_in[:, qs, :] = l
-            return carry
-
-        lax.fori_loop(0, half // 16, normalise, 0)
-        for i in range(8 // per):
-            k = g * (8 // per) + i
-            for t in range(0, per, 2):
-                pick = slice(i * per + t, i * per + t + 2)
-                h = high_in[pick].reshape(2 * half, NCHI)
-                l = low_in[pick].reshape(2 * half, NCHI)
-                spectra[k, :, t * half:(t + 2) * half] = (
-                    dot(high_ref[...], h, NT) + dot(high_ref[...], l, NT) + dot(low_ref[...], h, NT)
-                )
-            ring_copy(k, 0).start()
-        return carry
-
-    lax.fori_loop(0, frames // 8, transform, 0)
+    def transform(k, carry):
+        for t in range(0, per, 2):
+            cakes = raw[pl.ds(k * per + t, 2)] * inverse[...][None]
+            h, l = halves(cakes.reshape(2 * half, NCHI))
+            spectra[k, :, t * half:(t + 2) * half] = (
+                dot(high_ref[...], h, NT) + dot(high_ref[...], l, NT) + dot(low_ref[...], h, NT)
+            )
+        ring_copy(k, 0).start()
+        return carry
+
+    lax.fori_loop(0, SUBS, transform, 0)
 
     def take(k, s):
         sign = 1 - 2 * (k % 2)
@@ -354,7 +359,7 @@
             z_copy(g, d).start()
             return carry
 
-        lax.fori_loop(1, groups, z_start, 0)
+        lax.fori_loop(1, groups, z_start, 0, unroll=UNROLL)
         fs = pl.ds(pl.multiple_of(g * 8, 8), 8)
         mine[fg, :, fs, :] = sent[pl.ds(2 * fg, 2), fs, :]
         return carry
@@ -394,12 +399,18 @@
         swap_copy(g).wait_recv()
         corr[1 - core] = corr[1 - core] + product(g, theirs)
 
+    def ring_done(n, carry):
+        ring_copy(n % SUBS, n // SUBS).wait_send()
+        return carry
+
+    lax.fori_loop(0, (chips - 1) * SUBS, ring_done, 0)
+
     def correlate(g, carry):
         def z_wait(d, carry):
             z_landing(g, d).wait_recv()
             return carry
 
-        lax.fori_loop(1, groups, z_wait, 0)
+        lax.fori_loop(1, groups, z_wait, 0, unroll=UNROLL)
         swap_copy(g).start()
         corr[core] = corr[core] + product(g, mine)
 
@@ -438,6 +449,15 @@
         return carry
 
     lax.fori_loop(0, blocks, out_start, 0)
+
+    for g in range(frames // 8):
+        swap_copy(g).wait_send()
+
+    def z_done(n, carry):
+        z_copy(n // (groups - 1), 1 + n % (groups - 1)).wait_send()
+        return carry
+
+    lax.fori_loop(0, frames // 8 * (groups - 1), z_done, 0)
 
     @pl.when(owner_core == core)
     def _():
@@ -458,21 +478,6 @@
 
     lax.fori_loop(0, blocks, out_wait, 0)
     out_ref[...] = landed[...]
-
-    for g in range(frames // 8):
-        swap_copy(g).wait_send()
-
-    def ring_done(n, carry):
-        ring_copy(n % SUBS, n // SUBS).wait_send()
-        return carry
-
-    lax.fori_loop(0, (chips - 1) * SUBS, ring_done, 0)
-
-    def z_done(n, carry):
-        z_copy(n // (groups - 1), 1 + n % (groups - 1)).wait_send()
-        return carry
-
-    lax.fori_loop(0, frames // 8 * (groups - 1), z_done, 0)
 
 
 def linked(cake, counts, chips, groups):
@@ -498,8 +503,7 @@
             pltpu.VMEM((2 * NH, NCHI), bf),
             pltpu.VMEM((2 * NH, NCHI), bf),
             pltpu.VMEM((half, frames, NCHI), f32),
-            pltpu.VMEM((8, half, NCHI), bf),
-            pltpu.VMEM((8, half, NCHI), bf),
+            pltpu.VMEM((frames, half, NCHI), f32),
             pltpu.VMEM((SUBS, 2 * NH, per * half), f32),
             pltpu.VMEM((SUBS, chips - 1, rows, per * half), f32),
             pltpu.VMEM((devices, 8, NCHI), f32),

time: 101 us -> 96.2 us (0.952)
  Pallas kernels: 99.8 us -> 95.3 us
    pallas_call x1, Pallas kernels: 81.1 us -> 78.6 us  [linked(): pl.pallas_call(lambda *refs: link_kernel(chips, groups, *refs), out_shape...]
    pallas_call x1, Pallas kernels: 18.7 us -> 16.7 us  [binned(): pl.pallas_call(bin_kernel, out_shape=(jax.ShapeDtypeStruct((NQ, frames, N...]
where the time goes in v4:
time: 96.2 us
  Pallas kernels  95.3 us (99%)
    pallas_call x1, Pallas kernels, linked(): pl.pallas_call(lambda *refs: link_kernel(chips, groups, *refs), out_shape...  78.6 us
    pallas_call x1, Pallas kernels, binned(): pl.pallas_call(bin_kernel, out_shape=(jax.ShapeDtypeStruct((NQ, frames, N...  16.7 us

profile of v4, /device:TPU:1, one launch (start us, length us, event | category | flops | bytes accessed | tf_op | source)
XLA Modules:
  0.0 96.2 jit_solution(2183310300678310175)
XLA Ops:
  0.0 16.7 %binning.1 = (f32[256,32,256]{2,1,0:T(8,128)S(1)}, f32[256,256]{1,0:T(8,128)S(1)}) custom-call(s32[512]{0:T(512)} %rows_any.1, bf16[32,65536]{1,0:T(8,128)(2,1)} %x_any.1, s32[512,128]{1,0:T(8,128)} %bitcast.8, f32[512,128]{1,0:T(8,128)} %bitcast.9, s32[512,128]{1,0:T(8,128)} %bitcast.10), custom_call_target="tpu_custom_call" | custom-call | tf_op jit(solution)/shard_map/binning/pallas_call | solution.py:127
  16.7 78.6 %links.1 = f32[8,2,2,16,128]{4,3,2,1,0:T(8,128)S(1)} custom-call(f32[256,32,256]{2,1,0:T(8,128)S(1)} %get-tuple-element.7.refs_0_, f32[256,256]{1,0:T(8,128)S(1)} %get-tuple-element.8.refs_1_, bf16[256,256]{1,0:T(8,128)(2,1)} %constant.4.clone.refs_2_, bf16[256,256]{1,0:T(8,128)(2,1)} %constant.5.clone.refs_3_), custom_call_target="tpu_custom_call" | custom-call | tf_op jit(solution)/shard_map/links/pallas_call | solution.py:497
  95.3 0.9 copy.10

commit v5 on v4

--- a/solution.py
+++ b/solution.py
@@ -157,6 +157,10 @@
     return lax.dot_general(a, b, dims, preferred_element_type=jnp.float32)
 
 
+def far_first(d, n):
+    return 1 + (d - 1 + n // 2 - 1) % (n - 1)
+
+
 def link_kernel(
     chips, groups, cake_ref, count_ref, high_any, low_any, out_ref,
     high_ref, low_ref, other, raw, spectra, arrived, c1, c2, inverse,
@@ -186,11 +190,12 @@
     barrier = pltpu.get_barrier_semaphore()
 
     def greet(d, carry):
-        pl.semaphore_signal(barrier, inc=1, device_id=(fg, (p + d) % devices), device_id_type=MESH)
+        pl.semaphore_signal(barrier, inc=1, device_id=(fg, (p + far_first(d, devices)) % devices), device_id_type=MESH)
         return carry
 
     def greet_frames(d, carry):
-        pl.semaphore_signal(barrier, inc=1, device_id=((fg + d) % groups, p), device_id_type=MESH)
+        to = (fg + far_first(d, groups)) % groups
+        pl.semaphore_signal(barrier, inc=1, device_id=(to, p), device_id_type=MESH)
         return carry
 
     def greet_owners(i, carry):
@@ -217,7 +222,7 @@
         )
 
     def c1_start(d, carry):
-        c1_copy(d).start()
+        c1_copy(far_first(d, devices)).start()
         return carry
 
     lax.fori_loop(1, devices, c1_start, 0, unroll=UNROLL)
@@ -260,7 +265,7 @@
         )
 
     def c2_start(d, carry):
-        c2_copy(d).start()
+        c2_copy(far_first(d, groups)).start()
         return carry
 
     def c2_wait(d, carry):
@@ -356,7 +361,7 @@
             sent[t * 8:t * 8 + 8, pl.ds(pl.multiple_of(g * 8, 8), 8), :] = turned
 
         def z_start(d, carry):
-            z_copy(g, d).start()
+            z_copy(g, far_first(d, groups)).start()
             return carry
 
         lax.fori_loop(1, groups, z_start, 0, unroll=UNROLL)

time: 96.2 us -> 96.9 us (level)
  no operation moved by 1% of the time
where the time goes in v5:
time: 96.9 us; the launch traced here: 96.8 us
  Pallas kernels  95.9 us (99%)
    pallas_call x1, Pallas kernels, linked(): pl.pallas_call(lambda *refs: link_kernel(chips, groups, *refs), out_shape...  79.3 us
    pallas_call x1, Pallas kernels, binned(): pl.pallas_call(bin_kernel, out_shape=(jax.ShapeDtypeStruct((NQ, frames, N...  16.7 us

profile of v5, /device:TPU:1, one launch (start us, length us, event | category | flops | bytes accessed | tf_op | source)
XLA Modules:
  0.0 96.8 jit_solution(445897656538013927)
XLA Ops:
  0.0 16.7 %binning.1 = (f32[256,32,256]{2,1,0:T(8,128)S(1)}, f32[256,256]{1,0:T(8,128)S(1)}) custom-call(s32[512]{0:T(512)} %rows_any.1, bf16[32,65536]{1,0:T(8,128)(2,1)} %x_any.1, s32[512,128]{1,0:T(8,128)} %bitcast.8, f32[512,128]{1,0:T(8,128)} %bitcast.9, s32[512,128]{1,0:T(8,128)} %bitcast.10), custom_call_target="tpu_custom_call" | custom-call | tf_op jit(solution)/shard_map/binning/pallas_call | solution.py:127
  16.7 79.3 %links.1 = f32[8,2,2,16,128]{4,3,2,1,0:T(8,128)S(1)} custom-call(f32[256,32,256]{2,1,0:T(8,128)S(1)} %get-tuple-element.7.refs_0_, f32[256,256]{1,0:T(8,128)S(1)} %get-tuple-element.8.refs_1_, bf16[256,256]{1,0:T(8,128)(2,1)} %constant.4.clone.refs_2_, bf16[256,256]{1,0:T(8,128)(2,1)} %constant.5.clone.refs_3_), custom_call_target="tpu_custom_call" | custom-call | tf_op jit(solution)/shard_map/links/pallas_call | solution.py:502
  96.0 0.9 copy.10
